TPU v7x, 32 devices: a whole 2x2x4 slice. The times are simulated.
32 devices in a mesh: ctx: 8 (over z, x), heads: 4 (over y, core).
Axes of the slice: x: 2, y: 2, z: 4, core: 2. Of those that a mesh axis runs over, the one named last changes fastest.
Arguments:
- query_rows: bfloat16 [8, 16, 2, 128], P('ctx', 'heads'), may hold values from -6 to 6
- past_keys: bfloat16 [8, 16, 512, 128], P(None, 'heads', 'ctx'), may hold values from -6 to 6
- past_values: bfloat16 [8, 16, 512, 128], P(None, 'heads', 'ctx'), may hold values from -6 to 6
- used_length: int32 [8], replicated, may hold values from 256 to 512
Outputs:
- read: bfloat16 [8, 16, 2, 128], P('ctx', 'heads')
All inputs are finite; a program needn't handle non-finite values.
Results may differ from a plain program's by a relative error of at most 0.0015.
Values may be sent and summed in bfloat16 or wider, within the bound.
A program may use at most 64 MiB of HBM per device.

v0:
```python
import jax
import jax.numpy as jnp
from jax import lax
from jax.sharding import PartitionSpec as P

HEAD_SIZE = 128


def local(query_rows, past_keys, past_values, used_length):
    all_queries = lax.all_gather(query_rows, "ctx", axis=0, tiled=True)
    logit = jnp.einsum(
        "bkgd,bktd->bkgt", all_queries, past_keys, preferred_element_type=jnp.float32
    ) * HEAD_SIZE ** (-0.5)
    positions = lax.axis_index("ctx") * past_keys.shape[2] + jnp.arange(past_keys.shape[2])
    filled = positions[None, :] < used_length[:, None]
    logit = jnp.where(filled[:, None, None, :], logit, -1e30)
    top = jnp.max(logit, axis=-1)
    part = jnp.where(filled[:, None, None, :], jnp.exp(logit - top[..., None]), 0.0)
    weight_sum = jnp.sum(part, axis=-1)
    read_sum = jnp.einsum(
        "bkgt,bktd->bkgd", part, past_values.astype(jnp.float32), precision=lax.Precision.HIGHEST
    )
    tops, sums, parts = (
        lax.all_to_all(top[None], "ctx", split_axis=1, concat_axis=0, tiled=True),
        lax.all_to_all(weight_sum[None], "ctx", split_axis=1, concat_axis=0, tiled=True),
        lax.all_to_all(read_sum[None], "ctx", split_axis=1, concat_axis=0, tiled=True),
    )
    best = jnp.max(tops, axis=0)
    scale = jnp.exp(tops - best)
    weight_own = jnp.sum(sums * scale, axis=0)
    read_own = jnp.sum(parts * scale[..., None], axis=0)
    read = (read_own / weight_own[..., None]).astype(jnp.bfloat16)
    return read


def solution(mesh):
    return jax.shard_map(
        local,
        mesh=mesh,
        in_specs=(
            P("ctx", "heads", None, None),
            P(None, "heads", "ctx", None),
            P(None, "heads", "ctx", None),
            P(),
        ),
        out_specs=P("ctx", "heads", None, None),
        check_vma=False,
    )
```

profile of v0, /device:TPU:0, one launch (start us, length us, event | category | flops | bytes accessed | tf_op | source)
XLA Modules:
  0.0 62.1 jit_solution(10074065572557208397)
XLA Ops:
  0.0 0.0 copy-start
  0.0 0.0 copy-start.1
  0.0 0.7 %copy-done.1 = bf16[1,4,2,128]{3,2,1,0:T(2,128)(2,1)S(1)} copy-done((bf16[1,4,2,128]{3,2,1,0:T(2,128)(2,1)S(1)}, bf16[1,4,2,128]{3,2,1,0:T(2,128)(2,1)}, u32[]{:S(2)}) %copy-start.1) | copy-done | bytes 2072
  0.7 0.0 copy-start.2
  0.8 28.1 %all_gather.3 = bf16[8,4,2,128]{3,1,2,0:T(4,128)(2,1)S(1)} all-gather(bf16[1,4,2,128]{3,1,2,0:T(4,128)(2,1)S(1)} %copy.7), channel_id=1, replica_groups=mesh['ctx'=8,'heads'=4] {'ctx'}, dimensions={0}, use_global_device_ids=true | all-gather | bytes 18432 | tf_op jit(solution)/shard_map/all_gather | solution.py:10
  28.8 0.0 copy-done.2
  28.8 0.1 broadcast_compare_fusion
  28.9 1.5 %fusion.10 = (f32[8,4,2]{2,1,0:T(4,128)S(1)}, f32[8,4,2,64]{3,2,1,0:T(2,128)S(1)}) fusion(bf16[8,4,64,128]{3,2,1,0:T(8,128)(2,1)} %param.5, bf16[8,4,2,128]{3,1,2,0:T(4,128)(2,1)S(1)} %all_gather.3, pred[8,64]{1,0:T(8,128)(4,1)S(1)} %broadcast_compare_fusion), kind=kOutput, calls=%fused_computation.19 | convolution fusion | flops 1060800 | bytes 557824 | tf_op jit(solution)/shard_map/bkgd,bktd->bkgt/dot_general | solution.py:11
  30.4 0.7 %copy.11 = f32[1,8,4,2]{2,3,0,1:T(2,128)} copy(f32[1,8,4,2]{3,2,1,0:T(4,128)S(1)} %bitcast.30) | data formatting | bytes 512 | tf_op jit(solution)/shard_map/broadcast_in_dim | solution.py:24
  31.1 4.0 %all-to-all-start.1 = ((f32[1,8,4,2]{2,3,0,1:T(2,128)}), f32[1,8,4,2]{2,3,0,1:T(2,128)S(1)}, u32[]{:S(2)}, u32[]{:S(2)}) async-start(f32[1,8,4,2]{2,3,0,1:T(2,128)} %copy.11), calls=%async_computation.1 | async-start | bytes 16384 | tf_op jit(solution)/shard_map/all_to_all | solution.py:24
  35.1 0.0 copy-done
  35.1 1.2 %convolution_bitcast_fusion = f32[1,8,4,2,128]{4,3,2,0,1:T(2,128)} fusion(bf16[8,4,64,128]{3,2,1,0:T(8,128)(2,1)S(1)} %copy-done, f32[8,4,2,64]{3,2,1,0:T(2,128)S(1)} %get-tuple-element.6, pred[8,64]{1,0:T(8,128)(4,1)S(1)} %broadcast_compare_fusion, f32[8,4,2]{2,1,0:T(4,128)S(1)} %get-tuple-element.5), kind=kOutput, calls=%fused_computation | convolution fusion | flops 6299648 | bytes 574208 | tf_op jit(solution)/shard_map/bkgt,bktd->bkgd/dot_general | solution.py:20
  36.3 0.2 fusion.8
  36.5 0.7 %copy.15 = f32[1,8,4,2]{2,3,0,1:T(2,128)} copy(f32[1,8,4,2]{3,2,1,0:T(4,128)S(1)} %bitcast.31) | data formatting | bytes 512 | tf_op jit(solution)/shard_map/broadcast_in_dim | solution.py:25
  37.2 4.4 %all-to-all-done.1 = f32[1,8,4,2]{2,3,0,1:T(2,128)S(1)} async-done(((f32[1,8,4,2]{2,3,0,1:T(2,128)}), f32[1,8,4,2]{2,3,0,1:T(2,128)S(1)}, u32[]{:S(2)}, u32[]{:S(2)}) %all-to-all-start.1) | async-done | bytes 288 | tf_op jit(solution)/shard_map/all_to_all | solution.py:24
  41.6 3.3 %all-to-all-start.2 = ((f32[1,8,4,2]{2,3,0,1:T(2,128)}), f32[1,8,4,2]{2,3,0,1:T(2,128)S(1)}, u32[]{:S(2)}, u32[]{:S(2)}) async-start(f32[1,8,4,2]{2,3,0,1:T(2,128)} %copy.15), calls=%async_computation.2 | async-start | bytes 16384 | tf_op jit(solution)/shard_map/all_to_all | solution.py:25
  44.9 0.1 copy.12
  45.0 0.1 fusion.6
  45.1 6.3 %all-to-all-done.2 = f32[1,8,4,2]{2,3,0,1:T(2,128)S(1)} async-done(((f32[1,8,4,2]{2,3,0,1:T(2,128)}), f32[1,8,4,2]{2,3,0,1:T(2,128)S(1)}, u32[]{:S(2)}, u32[]{:S(2)}) %all-to-all-start.2) | async-done | bytes 288 | tf_op jit(solution)/shard_map/all_to_all | solution.py:25
  51.4 3.3 %all-to-all-start = ((f32[1,8,4,2,128]{4,3,2,0,1:T(2,128)}), f32[1,8,4,2,128]{4,3,2,0,1:T(2,128)S(1)}, u32[]{:S(2)}, u32[]{:S(2)}) async-start(f32[1,8,4,2,128]{4,3,2,0,1:T(2,128)} %convolution_bitcast_fusion), calls=%async_computation | async-start | bytes 65536 | tf_op jit(solution)/shard_map/all_to_all | solution.py:26
  54.7 0.1 copy.16
  54.8 0.2 fusion.5
  55.0 0.1 copy.18
  55.1 0.1 copy.13
  55.2 6.2 %all-to-all-done = f32[1,8,4,2,128]{4,3,2,0,1:T(2,128)S(1)} async-done(((f32[1,8,4,2,128]{4,3,2,0,1:T(2,128)}), f32[1,8,4,2,128]{4,3,2,0,1:T(2,128)S(1)}, u32[]{:S(2)}, u32[]{:S(2)}) %all-to-all-start) | async-done | bytes 32800 | tf_op jit(solution)/shard_map/all_to_all | solution.py:26
  61.4 0.1 fusion.1
  61.5 0.7 %fusion.7 = bf16[1,4,2,128]{3,2,1,0:T(2,128)(2,1)} fusion(f32[4,2,128]{2,1,0:T(2,128)S(1)} %fusion.1, f32[4,2]{1,0:T(4,128)S(1)} %copy.18), kind=kLoop, calls=%fused_computation.14 | loop fusion | flops 2048 | bytes 6176 | tf_op jit(solution)/shard_map/convert_element_type | solution.py:32
  (3 shorter events, 0.0 us)
Async XLA Ops:
  0.0 35.1 %copy-start = (bf16[8,4,64,128]{3,2,1,0:T(8,128)(2,1)S(1)}, bf16[8,4,64,128]{3,2,1,0:T(8,128)(2,1)}, u32[]{:S(2)}) copy-start(bf16[8,4,64,128]{3,2,1,0:T(8,128)(2,1)} %param.6) | copy-start | bytes 1572868
  0.0 0.7 %copy-start.1 = (bf16[1,4,2,128]{3,2,1,0:T(2,128)(2,1)S(1)}, bf16[1,4,2,128]{3,2,1,0:T(2,128)(2,1)}, u32[]{:S(2)}) copy-start(bf16[1,4,2,128]{3,2,1,0:T(2,128)(2,1)} %param.4) | copy-start | bytes 6148
  0.7 28.1 %copy-start.2 = (s32[8]{0:T(128)S(1)}, s32[8]{0:T(128)}, u32[]{:S(2)}) copy-start(s32[8]{0:T(128)} %param.7) | copy-start | bytes 100
  31.1 10.5 %all-to-all-start.1 = ((f32[1,8,4,2]{2,3,0,1:T(2,128)}), f32[1,8,4,2]{2,3,0,1:T(2,128)S(1)}, u32[]{:S(2)}, u32[]{:S(2)}) async-start(f32[1,8,4,2]{2,3,0,1:T(2,128)} %copy.11), calls=%async_computation.1 | async-start | bytes 16384 | tf_op jit(solution)/shard_map/all_to_all | solution.py:24
  41.6 9.8 %all-to-all-start.2 = ((f32[1,8,4,2]{2,3,0,1:T(2,128)}), f32[1,8,4,2]{2,3,0,1:T(2,128)S(1)}, u32[]{:S(2)}, u32[]{:S(2)}) async-start(f32[1,8,4,2]{2,3,0,1:T(2,128)} %copy.15), calls=%async_computation.2 | async-start | bytes 16384 | tf_op jit(solution)/shard_map/all_to_all | solution.py:25
  51.4 10.0 %all-to-all-start = ((f32[1,8,4,2,128]{4,3,2,0,1:T(2,128)}), f32[1,8,4,2,128]{4,3,2,0,1:T(2,128)S(1)}, u32[]{:S(2)}, u32[]{:S(2)}) async-start(f32[1,8,4,2,128]{4,3,2,0,1:T(2,128)} %convolution_bitcast_fusion), calls=%async_computation | async-start | bytes 65536 | tf_op jit(solution)/shard_map/all_to_all | solution.py:26
where the time goes:
time: 62.5 us; the launch traced here: 62.1 us
  blocking collectives  28.1 us (45%)
  waiting for transfers between devices  16.8 us (27%)
  starting transfers between devices  10.6 us (17%)
  matrix products  2.71 us (4%)
  local copies, waits for them, and re-layouts  2.59 us (4%)
  other arithmetic  1.32 us (2%)
    all_gather x1, blocking collectives, local(): all_queries = lax.all_gather(query_rows, 'ctx', axis=0, tiled=True)  28.1 us
    all_to_all x1, waiting for transfers between devices, local(): lax.all_to_all(weight_sum[None], 'ctx', split_axis=1, concat_axis=0, tile...  6.27 us
    all_to_all x1, waiting for transfers between devices, local(): lax.all_to_all(read_sum[None], 'ctx', split_axis=1, concat_axis=0, tiled=...  6.17 us
    all_to_all x1, waiting for transfers between devices, local(): lax.all_to_all(top[None], 'ctx', split_axis=1, concat_axis=0, tiled=True)  4.37 us
    all_to_all x1, starting transfers between devices, local(): lax.all_to_all(top[None], 'ctx', split_axis=1, concat_axis=0, tiled=True)  3.97 us
    all_to_all x1, starting transfers between devices, local(): lax.all_to_all(read_sum[None], 'ctx', split_axis=1, concat_axis=0, tiled=...  3.33 us
    all_to_all x1, starting transfers between devices, local(): lax.all_to_all(weight_sum[None], 'ctx', split_axis=1, concat_axis=0, tile...  3.32 us
    dot_general x1, matrix products, local(): jnp.einsum('bkgd,bktd->bkgt', all_queries, past_keys, preferred_element_t...  1.51 us
  transfers between devices with their start and end apart: 3, of which 3 were waited for; matrix products, arithmetic and copies ran while one was open for 4% of the time, Pallas kernels for 0%

commit v1 on v0

--- a/solution.py
+++ b/solution.py
@@ -7,7 +7,22 @@
 
 
 def local(query_rows, past_keys, past_values, used_length):
-    all_queries = lax.all_gather(query_rows, "ctx", axis=0, tiled=True)
+    ways, here, step = (lax.axis_size("ctx"), lax.axis_index("ctx"), query_rows.shape[0])
+    shape = [n * ways if d == 0 else n for d, n in enumerate(query_rows.shape)]
+    all_queries = lax.dynamic_update_slice_in_dim(
+        jnp.zeros(shape, query_rows.dtype), query_rows, here * step, axis=0
+    )
+    going_up = going_down = query_rows
+    for far in range(1, ways // 2 + 1):
+        going_up = lax.ppermute(going_up, "ctx", [(d, (d + 1) % ways) for d in range(ways)])
+        all_queries = lax.dynamic_update_slice_in_dim(
+            all_queries, going_up, (here - far) % ways * step, axis=0
+        )
+        if 2 * far < ways:
+            going_down = lax.ppermute(going_down, "ctx", [(d, (d - 1) % ways) for d in range(ways)])
+            all_queries = lax.dynamic_update_slice_in_dim(
+                all_queries, going_down, (here + far) % ways * step, axis=0
+            )
     logit = jnp.einsum(
         "bkgd,bktd->bkgt", all_queries, past_keys, preferred_element_type=jnp.float32
     ) * HEAD_SIZE ** (-0.5)

time: 62.5 us -> 59.5 us (0.952)
  blocking collectives: 28.1 us -> 0 us
  starting transfers between devices: 10.6 us -> 25.6 us
  waiting for transfers between devices: 16.8 us -> 26.2 us
  local copies, waits for them, and re-layouts: 2.59 us -> 3.29 us
    all_gather x1 -> x0, blocking collectives: 28.1 us -> none  [local(): all_queries = lax.all_gather(query_rows, 'ctx', axis=0, tiled=True)]
    ppermute x0 -> x7, starting transfers between devices: none -> 15.6 us  [the longest x3 12.6 us: local(): lax.ppermute(going_down, 'ctx', [(d, (d - 1) % ways) for d in range(ways)])]
    ppermute x0 -> x7, waiting for transfers between devices: none -> 9.48 us  [the longest x4 9.47 us: local(): lax.ppermute(going_up, 'ctx', [(d, (d + 1) % ways) for d in range(ways)])]
    all_to_all x1, starting transfers between devices: 3.97 us -> 3.29 us  [local(): lax.all_to_all(top[None], 'ctx', split_axis=1, concat_axis=0, tiled=True)]
    unnamed x7 -> x6, local copies, waits for them, and re-layouts: 0.75 us -> 1.35 us
  transfers between devices with their start and end apart: 3 -> 10, of which waited for: 3 -> 7; matrix products, arithmetic and copies ran while one was open for 4% -> 5% of each run, Pallas kernels for 0% -> 0%
where the time goes in v1:
time: 59.5 us; the launch traced here: 59.1 us
  waiting for transfers between devices  26.2 us (44%)
  starting transfers between devices  25.6 us (43%)
  local copies, waits for them, and re-layouts  3.29 us (6%)
  matrix products  2.71 us (5%)
  other arithmetic  1.32 us (2%)
    ppermute x3, starting transfers between devices, local(): lax.ppermute(going_down, 'ctx', [(d, (d - 1) % ways) for d in range(ways)])  12.6 us
    ppermute x4, waiting for transfers between devices, local(): lax.ppermute(going_up, 'ctx', [(d, (d + 1) % ways) for d in range(ways)])  9.47 us
    all_to_all x1, waiting for transfers between devices, local(): lax.all_to_all(weight_sum[None], 'ctx', split_axis=1, concat_axis=0, tile...  6.27 us
    all_to_all x1, waiting for transfers between devices, local(): lax.all_to_all(read_sum[None], 'ctx', split_axis=1, concat_axis=0, tiled=...  6.17 us
    all_to_all x1, waiting for transfers between devices, local(): lax.all_to_all(top[None], 'ctx', split_axis=1, concat_axis=0, tiled=True)  4.29 us
    all_to_all x1, starting transfers between devices, local(): lax.all_to_all(read_sum[None], 'ctx', split_axis=1, concat_axis=0, tiled=...  3.33 us
    all_to_all x1, starting transfers between devices, local(): lax.all_to_all(weight_sum[None], 'ctx', split_axis=1, concat_axis=0, tile...  3.32 us
    all_to_all x1, starting transfers between devices, local(): lax.all_to_all(top[None], 'ctx', split_axis=1, concat_axis=0, tiled=True)  3.29 us
  transfers between devices with their start and end apart: 10, of which 7 were waited for; matrix products, arithmetic and copies ran while one was open for 5% of the time, Pallas kernels for 0%

profile of v1, /device:TPU:0, one launch (start us, length us, event | category | flops | bytes accessed | tf_op | source)
XLA Modules:
  0.0 59.1 jit_solution(1120090613743013736)
XLA Ops:
  0.0 0.0 copy-start
  0.0 3.0 %collective-permute-start = (bf16[1,4,2,128]{3,2,1,0:T(2,128)(2,1)}, bf16[1,4,2,128]{3,2,1,0:T(2,128)(2,1)S(1)}, u32[]{:S(2)}, u32[]{:S(2)}) collective-permute-start(bf16[1,4,2,128]{3,2,1,0:T(2,128)(2,1)} %param.4), channel_id=1, source_target_pairs={{0,4},{4,8},{8,12},{12,16},{16,20},{20,24},{24,28},{28,0},{1,5},{5... | collective-permute-start | bytes 6152 | tf_op jit(solution)/shard_map/ppermute | solution.py:17
  3.0 3.1 %collective-permute-start.1 = (bf16[1,4,2,128]{3,2,1,0:T(2,128)(2,1)}, bf16[1,4,2,128]{3,2,1,0:T(2,128)(2,1)S(1)}, u32[]{:S(2)}, u32[]{:S(2)}) collective-permute-start(bf16[1,4,2,128]{3,2,1,0:T(2,128)(2,1)} %param.4), channel_id=1, source_target_pairs={{0,28},{4,0},{8,4},{12,8},{16,12},{20,16},{24,20},{28,24},{1,29},{... | collective-permute-start | bytes 6152 | tf_op jit(solution)/shard_map/ppermute | solution.py:22
  6.1 0.0 copy-start.1
  6.1 0.7 %copy-done.1 = bf16[1,4,2,128]{3,2,1,0:T(2,128)(2,1)S(1)} copy-done((bf16[1,4,2,128]{3,2,1,0:T(2,128)(2,1)S(1)}, bf16[1,4,2,128]{3,2,1,0:T(2,128)(2,1)}, u32[]{:S(2)}) %copy-start.1) | copy-done | bytes 2072
  6.8 0.0 copy-start.2
  6.8 0.6 %copy-done.2 = s32[8]{0:T(128)S(1)} copy-done((s32[8]{0:T(128)S(1)}, s32[8]{0:T(128)}, u32[]{:S(2)}) %copy-start.2) | copy-done | bytes 56
  7.4 0.1 broadcast_compare_fusion
  7.5 0.3 collective-permute-done
  7.8 0.0 collective-permute-start.2
  7.8 0.0 collective-permute-done.1
  7.8 4.8 %collective-permute-start.3 = (bf16[1,4,2,128]{3,2,1,0:T(2,128)(2,1)S(1)}, bf16[1,4,2,128]{3,2,1,0:T(2,128)(2,1)S(1)}, u32[]{:S(2)}, u32[]{:S(2)}) collective-permute-start(bf16[1,4,2,128]{3,2,1,0:T(2,128)(2,1)S(1)} %collective-permute-done.1), channel_id=1, source_target_pairs={{0,28},{4,0},{8,4},{12,8},{16,12},{20,16},{24,20},{28,24},{1,29},{... | collective-permute-start | bytes 6152 | tf_op jit(solution)/shard_map/ppermute | solution.py:22
  12.6 1.5 %collective-permute-done.2 = bf16[1,4,2,128]{3,2,1,0:T(2,128)(2,1)S(1)} collective-permute-done((bf16[1,4,2,128]{3,2,1,0:T(2,128)(2,1)S(1)}, bf16[1,4,2,128]{3,2,1,0:T(2,128)(2,1)S(1)}, u32[]{:S(2)}, u32[]{:S(2)}) %collective-permute-start.2) | collective-permute-done | bytes 2080 | tf_op jit(solution)/shard_map/ppermute | solution.py:17
  14.1 0.0 collective-permute-start.4
  14.1 0.0 collective-permute-done.3
  14.1 4.8 %collective-permute-start.5 = (bf16[1,4,2,128]{3,2,1,0:T(2,128)(2,1)S(1)}, bf16[1,4,2,128]{3,2,1,0:T(2,128)(2,1)S(1)}, u32[]{:S(2)}, u32[]{:S(2)}) collective-permute-start(bf16[1,4,2,128]{3,2,1,0:T(2,128)(2,1)S(1)} %collective-permute-done.3), channel_id=1, source_target_pairs={{0,28},{4,0},{8,4},{12,8},{16,12},{20,16},{24,20},{28,24},{1,29},{... | collective-permute-start | bytes 6152 | tf_op jit(solution)/shard_map/ppermute | solution.py:22
  18.9 1.5 %collective-permute-done.4 = bf16[1,4,2,128]{3,2,1,0:T(2,128)(2,1)S(1)} collective-permute-done((bf16[1,4,2,128]{3,2,1,0:T(2,128)(2,1)S(1)}, bf16[1,4,2,128]{3,2,1,0:T(2,128)(2,1)S(1)}, u32[]{:S(2)}, u32[]{:S(2)}) %collective-permute-start.4) | collective-permute-done | bytes 2080 | tf_op jit(solution)/shard_map/ppermute | solution.py:17
  20.3 0.0 collective-permute-start.6
  20.4 0.0 collective-permute-done.5
  20.4 6.2 %collective-permute-done.6 = bf16[1,4,2,128]{3,2,1,0:T(2,128)(2,1)S(1)} collective-permute-done((bf16[1,4,2,128]{3,2,1,0:T(2,128)(2,1)S(1)}, bf16[1,4,2,128]{3,2,1,0:T(2,128)(2,1)S(1)}, u32[]{:S(2)}, u32[]{:S(2)}) %collective-permute-start.6) | collective-permute-done | bytes 2080 | tf_op jit(solution)/shard_map/ppermute | solution.py:17
  26.6 1.5 %fusion.9 = (f32[8,4,2]{2,1,0:T(4,128)S(1)}, f32[8,4,2,64]{3,2,1,0:T(2,128)S(1)}) fusion(bf16[8,4,2,128]{3,2,1,0:T(2,128)(2,1)S(1)} %constant_dynamic-update-slice_fusion, bf16[8,4,64,128]{3,2,1,0:T(8,128)(2,1)} %param.5, pred[8,64]{1,0:T(8,128)(4,1)S(1)} %broadcast_compare_fusion), kind=kOutput, calls=%fused_computation.26 | convolution fusion | flops 1060800 | bytes 557824 | tf_op jit(solution)/shard_map/bkgd,bktd->bkgt/dot_general | solution.py:26
  28.1 0.7 %copy.9 = f32[1,8,4,2]{2,3,0,1:T(2,128)} copy(f32[1,8,4,2]{3,2,1,0:T(4,128)S(1)} %bitcast.31) | data formatting | bytes 512 | tf_op jit(solution)/shard_map/broadcast_in_dim | solution.py:39
  28.9 3.3 %all-to-all-start.1 = ((f32[1,8,4,2]{2,3,0,1:T(2,128)}), f32[1,8,4,2]{2,3,0,1:T(2,128)S(1)}, u32[]{:S(2)}, u32[]{:S(2)}) async-start(f32[1,8,4,2]{2,3,0,1:T(2,128)} %copy.9), calls=%async_computation.1 | async-start | bytes 16384 | tf_op jit(solution)/shard_map/all_to_all | solution.py:39
  32.2 0.0 copy-done
  32.2 1.2 %convolution_bitcast_fusion = f32[1,8,4,2,128]{4,3,2,0,1:T(2,128)} fusion(bf16[8,4,64,128]{3,2,1,0:T(8,128)(2,1)S(1)} %copy-done, f32[8,4,2,64]{3,2,1,0:T(2,128)S(1)} %get-tuple-element.6, pred[8,64]{1,0:T(8,128)(4,1)S(1)} %broadcast_compare_fusion, f32[8,4,2]{2,1,0:T(4,128)S(1)} %get-tuple-element.5), kind=kOutput, calls=%fused_computation | convolution fusion | flops 6299648 | bytes 574208 | tf_op jit(solution)/shard_map/bkgt,bktd->bkgd/dot_general | solution.py:35
  33.4 0.2 fusion.7
  33.6 0.7 %copy.13 = f32[1,8,4,2]{2,3,0,1:T(2,128)} copy(f32[1,8,4,2]{3,2,1,0:T(4,128)S(1)} %bitcast.32) | data formatting | bytes 512 | tf_op jit(solution)/shard_map/broadcast_in_dim | solution.py:40
  34.3 4.3 %all-to-all-done.1 = f32[1,8,4,2]{2,3,0,1:T(2,128)S(1)} async-done(((f32[1,8,4,2]{2,3,0,1:T(2,128)}), f32[1,8,4,2]{2,3,0,1:T(2,128)S(1)}, u32[]{:S(2)}, u32[]{:S(2)}) %all-to-all-start.1) | async-done | bytes 288 | tf_op jit(solution)/shard_map/all_to_all | solution.py:39
  38.6 3.3 %all-to-all-start.2 = ((f32[1,8,4,2]{2,3,0,1:T(2,128)}), f32[1,8,4,2]{2,3,0,1:T(2,128)S(1)}, u32[]{:S(2)}, u32[]{:S(2)}) async-start(f32[1,8,4,2]{2,3,0,1:T(2,128)} %copy.13), calls=%async_computation.2 | async-start | bytes 16384 | tf_op jit(solution)/shard_map/all_to_all | solution.py:40
  42.0 0.1 copy.10
  42.1 0.1 fusion.5
  42.1 6.3 %all-to-all-done.2 = f32[1,8,4,2]{2,3,0,1:T(2,128)S(1)} async-done(((f32[1,8,4,2]{2,3,0,1:T(2,128)}), f32[1,8,4,2]{2,3,0,1:T(2,128)S(1)}, u32[]{:S(2)}, u32[]{:S(2)}) %all-to-all-start.2) | async-done | bytes 288 | tf_op jit(solution)/shard_map/all_to_all | solution.py:40
  48.4 3.3 %all-to-all-start = ((f32[1,8,4,2,128]{4,3,2,0,1:T(2,128)}), f32[1,8,4,2,128]{4,3,2,0,1:T(2,128)S(1)}, u32[]{:S(2)}, u32[]{:S(2)}) async-start(f32[1,8,4,2,128]{4,3,2,0,1:T(2,128)} %convolution_bitcast_fusion), calls=%async_computation | async-start | bytes 65536 | tf_op jit(solution)/shard_map/all_to_all | solution.py:41
  51.8 0.1 copy.14
  51.8 0.2 fusion.4
  52.0 0.1 copy.16
  52.1 0.1 copy.11
  52.2 6.2 %all-to-all-done = f32[1,8,4,2,128]{4,3,2,0,1:T(2,128)S(1)} async-done(((f32[1,8,4,2,128]{4,3,2,0,1:T(2,128)}), f32[1,8,4,2,128]{4,3,2,0,1:T(2,128)S(1)}, u32[]{:S(2)}, u32[]{:S(2)}) %all-to-all-start) | async-done | bytes 32800 | tf_op jit(solution)/shard_map/all_to_all | solution.py:41
  58.4 0.1 fusion.1
  58.5 0.7 %fusion.6 = bf16[1,4,2,128]{3,2,1,0:T(2,128)(2,1)} fusion(f32[4,2,128]{2,1,0:T(2,128)S(1)} %fusion.1, f32[4,2]{1,0:T(4,128)S(1)} %copy.16), kind=kLoop, calls=%fused_computation.13 | loop fusion | flops 2048 | bytes 6176 | tf_op jit(solution)/shard_map/convert_element_type | solution.py:47
  (11 shorter events, 0.1 us)
Async XLA Ops:
  0.0 32.2 %copy-start = (bf16[8,4,64,128]{3,2,1,0:T(8,128)(2,1)S(1)}, bf16[8,4,64,128]{3,2,1,0:T(8,128)(2,1)}, u32[]{:S(2)}) copy-start(bf16[8,4,64,128]{3,2,1,0:T(8,128)(2,1)} %param.6) | copy-start | bytes 1572868
  0.0 7.8 %collective-permute-start = (bf16[1,4,2,128]{3,2,1,0:T(2,128)(2,1)}, bf16[1,4,2,128]{3,2,1,0:T(2,128)(2,1)S(1)}, u32[]{:S(2)}, u32[]{:S(2)}) collective-permute-start(bf16[1,4,2,128]{3,2,1,0:T(2,128)(2,1)} %param.4), channel_id=1, source_target_pairs={{0,4},{4,8},{8,12},{12,16},{16,20},{20,24},{24,28},{28,0},{1,5},{5... | collective-permute-start | bytes 6152 | tf_op jit(solution)/shard_map/ppermute | solution.py:17
  3.0 4.8 %collective-permute-start.1 = (bf16[1,4,2,128]{3,2,1,0:T(2,128)(2,1)}, bf16[1,4,2,128]{3,2,1,0:T(2,128)(2,1)S(1)}, u32[]{:S(2)}, u32[]{:S(2)}) collective-permute-start(bf16[1,4,2,128]{3,2,1,0:T(2,128)(2,1)} %param.4), channel_id=1, source_target_pairs={{0,28},{4,0},{8,4},{12,8},{16,12},{20,16},{24,20},{28,24},{1,29},{... | collective-permute-start | bytes 6152 | tf_op jit(solution)/shard_map/ppermute | solution.py:22
  6.1 0.7 %copy-start.1 = (bf16[1,4,2,128]{3,2,1,0:T(2,128)(2,1)S(1)}, bf16[1,4,2,128]{3,2,1,0:T(2,128)(2,1)}, u32[]{:S(2)}) copy-start(bf16[1,4,2,128]{3,2,1,0:T(2,128)(2,1)} %param.4) | copy-start | bytes 6148
  6.8 0.7 %copy-start.2 = (s32[8]{0:T(128)S(1)}, s32[8]{0:T(128)}, u32[]{:S(2)}) copy-start(s32[8]{0:T(128)} %param.7) | copy-start | bytes 100
  7.8 6.3 %collective-permute-start.2 = (bf16[1,4,2,128]{3,2,1,0:T(2,128)(2,1)S(1)}, bf16[1,4,2,128]{3,2,1,0:T(2,128)(2,1)S(1)}, u32[]{:S(2)}, u32[]{:S(2)}) collective-permute-start(bf16[1,4,2,128]{3,2,1,0:T(2,128)(2,1)S(1)} %collective-permute-done), channel_id=1, source_target_pairs={{0,4},{4,8},{8,12},{12,16},{16,20},{20,24},{24,28},{28,0},{1,5},{5... | collective-permute-start | bytes 6152 | tf_op jit(solution)/shard_map/ppermute | solution.py:17
  7.8 6.3 %collective-permute-start.3 = (bf16[1,4,2,128]{3,2,1,0:T(2,128)(2,1)S(1)}, bf16[1,4,2,128]{3,2,1,0:T(2,128)(2,1)S(1)}, u32[]{:S(2)}, u32[]{:S(2)}) collective-permute-start(bf16[1,4,2,128]{3,2,1,0:T(2,128)(2,1)S(1)} %collective-permute-done.1), channel_id=1, source_target_pairs={{0,28},{4,0},{8,4},{12,8},{16,12},{20,16},{24,20},{28,24},{1,29},{... | collective-permute-start | bytes 6152 | tf_op jit(solution)/shard_map/ppermute | solution.py:22
  14.1 6.3 %collective-permute-start.4 = (bf16[1,4,2,128]{3,2,1,0:T(2,128)(2,1)S(1)}, bf16[1,4,2,128]{3,2,1,0:T(2,128)(2,1)S(1)}, u32[]{:S(2)}, u32[]{:S(2)}) collective-permute-start(bf16[1,4,2,128]{3,2,1,0:T(2,128)(2,1)S(1)} %collective-permute-done.2), channel_id=1, source_target_pairs={{0,4},{4,8},{8,12},{12,16},{16,20},{20,24},{24,28},{28,0},{1,5},{5... | collective-permute-start | bytes 6152 | tf_op jit(solution)/shard_map/ppermute | solution.py:17
  14.1 6.3 %collective-permute-start.5 = (bf16[1,4,2,128]{3,2,1,0:T(2,128)(2,1)S(1)}, bf16[1,4,2,128]{3,2,1,0:T(2,128)(2,1)S(1)}, u32[]{:S(2)}, u32[]{:S(2)}) collective-permute-start(bf16[1,4,2,128]{3,2,1,0:T(2,128)(2,1)S(1)} %collective-permute-done.3), channel_id=1, source_target_pairs={{0,28},{4,0},{8,4},{12,8},{16,12},{20,16},{24,20},{28,24},{1,29},{... | collective-permute-start | bytes 6152 | tf_op jit(solution)/shard_map/ppermute | solution.py:22
  20.3 6.3 %collective-permute-start.6 = (bf16[1,4,2,128]{3,2,1,0:T(2,128)(2,1)S(1)}, bf16[1,4,2,128]{3,2,1,0:T(2,128)(2,1)S(1)}, u32[]{:S(2)}, u32[]{:S(2)}) collective-permute-start(bf16[1,4,2,128]{3,2,1,0:T(2,128)(2,1)S(1)} %collective-permute-done.4), channel_id=1, source_target_pairs={{0,4},{4,8},{8,12},{12,16},{16,20},{20,24},{24,28},{28,0},{1,5},{5... | collective-permute-start | bytes 6152 | tf_op jit(solution)/shard_map/ppermute | solution.py:17
  28.9 9.8 %all-to-all-start.1 = ((f32[1,8,4,2]{2,3,0,1:T(2,128)}), f32[1,8,4,2]{2,3,0,1:T(2,128)S(1)}, u32[]{:S(2)}, u32[]{:S(2)}) async-start(f32[1,8,4,2]{2,3,0,1:T(2,128)} %copy.9), calls=%async_computation.1 | async-start | bytes 16384 | tf_op jit(solution)/shard_map/all_to_all | solution.py:39
  38.6 9.8 %all-to-all-start.2 = ((f32[1,8,4,2]{2,3,0,1:T(2,128)}), f32[1,8,4,2]{2,3,0,1:T(2,128)S(1)}, u32[]{:S(2)}, u32[]{:S(2)}) async-start(f32[1,8,4,2]{2,3,0,1:T(2,128)} %copy.13), calls=%async_computation.2 | async-start | bytes 16384 | tf_op jit(solution)/shard_map/all_to_all | solution.py:40
  48.4 10.0 %all-to-all-start = ((f32[1,8,4,2,128]{4,3,2,0,1:T(2,128)}), f32[1,8,4,2,128]{4,3,2,0,1:T(2,128)S(1)}, u32[]{:S(2)}, u32[]{:S(2)}) async-start(f32[1,8,4,2,128]{4,3,2,0,1:T(2,128)} %convolution_bitcast_fusion), calls=%async_computation | async-start | bytes 65536 | tf_op jit(solution)/shard_map/all_to_all | solution.py:41
